TPU v7x, 16 devices: a 4x2x1 block of a 4x4x8 slice. The times are simulated.
16 devices in a mesh: dp: 2 (over y, z), cp: 8 (over x, core).
Axes of the slice: x: 4, y: 2, z: 1, core: 2. Of those that a mesh axis runs over, the one named last changes fastest.
The devices are a block of a 4x4x8 slice.
Arguments:
- images: bfloat16 [32, 1024, 768], P('dp', 'cp'), parts along dimension 0
- ln1_scale: float32 [768], replicated
- ln1_bias: float32 [768], replicated
- w_qkv: bfloat16 [768, 3, 12, 64], replicated
- b_qkv: float32 [3, 12, 64], replicated
- w_out: bfloat16 [12, 64, 768], replicated
- b_out: float32 [768], replicated
- ln2_scale: float32 [768], replicated
- ln2_bias: float32 [768], replicated
- w_up: bfloat16 [768, 3072], replicated
- b_up: float32 [3072], replicated
- w_down: bfloat16 [3072, 768], replicated
- b_down: float32 [768], replicated
- lnf_scale: float32 [768], replicated
- lnf_bias: float32 [768], replicated
- pool_probe: bfloat16 [1, 768], replicated
- pool_wq: bfloat16 [768, 12, 64], replicated
- pool_bq: float32 [12, 64], replicated
- pool_wkv: bfloat16 [768, 2, 12, 64], replicated
- pool_bkv: float32 [2, 12, 64], replicated
- pool_wout: bfloat16 [12, 64, 768], replicated
- pool_bout: float32 [768], replicated
- pool_ln_scale: float32 [768], replicated
- pool_ln_bias: float32 [768], replicated
- pool_w_up: bfloat16 [768, 3072], replicated
- pool_b_up: float32 [3072], replicated
- pool_w_down: bfloat16 [3072, 768], replicated
- pool_b_down: float32 [768], replicated
Outputs:
- output: float32 [32, 768], P('dp'), parts along dimension 0
There are 2 independent parts. A program takes and returns all parts, laid end to end along the dimension named above; an argument that names none is the same for every part.
All inputs are finite; a program needn't handle non-finite values.
Results may differ from a plain program's by a relative error of at most 0.0093231.
Values are sent between devices in bfloat16 or wider.
A program may use at most 768 MiB of HBM per device.

v0:
```python
import jax
import jax.numpy as jnp
from jax import lax
from jax.sharding import PartitionSpec as P

EPSILON = 1e-6


def layer_norm(values, ln_gain, ln_shift):
    row_mean = jnp.mean(values, axis=-1, keepdims=True)
    centered = values - row_mean
    variance = jnp.mean(centered * centered, axis=-1, keepdims=True)
    return centered * lax.rsqrt(variance + EPSILON) * ln_gain + ln_shift


def project(normed, weight, bias_vec):
    return (jnp.einsum("bnd,dhe->bnhe", normed, weight, preferred_element_type=jnp.float32) + bias_vec).astype(jnp.bfloat16)


def block_stats(queries, key_rows, value_rows, score_scale):
    scores = jnp.einsum("bqhe,bkhe->bhqk", queries, key_rows, preferred_element_type=jnp.float32) * score_scale
    row_max = jnp.max(scores, axis=-1)
    weights = jnp.exp(scores - row_max[..., None])
    value_sum = jnp.einsum("bhqk,bkhe->bhqe", weights.astype(jnp.bfloat16), value_rows, preferred_element_type=jnp.float32)
    return row_max, jnp.sum(weights, axis=-1), value_sum


def merge_stats(first_stats, second_stats):
    first_max, first_sum, first_val = first_stats
    second_max, second_sum, second_val = second_stats
    joint_max = jnp.maximum(first_max, second_max)
    first_factor = jnp.exp(first_max - joint_max)
    second_factor = jnp.exp(second_max - joint_max)
    joint_sum = first_sum * first_factor + second_sum * second_factor
    joint_val = first_val * first_factor[..., None] + second_val * second_factor[..., None]
    return joint_max, joint_sum, joint_val


def token_tail(resid_in, context, w_out, b_out, ln2_scale, ln2_bias, w_up, b_up, w_down, b_down, lnf_scale, lnf_bias):
    attn_out = jnp.einsum("cirf,ife->cre", context, w_out, preferred_element_type=jnp.float32) + b_out
    resid_mid = (resid_in + attn_out).astype(jnp.bfloat16)
    normed_mid = layer_norm(resid_mid.astype(jnp.float32), ln2_scale, ln2_bias).astype(jnp.bfloat16)
    hidden = jax.nn.gelu(jnp.einsum("bnd,df->bnf", normed_mid, w_up, preferred_element_type=jnp.float32) + b_up, approximate=True).astype(jnp.bfloat16)
    layer_out = (resid_mid.astype(jnp.float32) + jnp.einsum("bnf,fd->bnd", hidden, w_down, preferred_element_type=jnp.float32) + b_down).astype(jnp.bfloat16)
    return layer_norm(layer_out.astype(jnp.float32), lnf_scale, lnf_bias).astype(jnp.bfloat16)


def pool_stats(tokens_out, pool_probe, pool_wq, pool_bq, pool_wkv, pool_bkv, score_scale):
    probe_q = (jnp.einsum("od,dhe->he", pool_probe, pool_wq, preferred_element_type=jnp.float32) + pool_bq).astype(jnp.bfloat16)
    pool_keys = project(tokens_out, pool_wkv[:, 0], pool_bkv[0])
    pool_vals = project(tokens_out, pool_wkv[:, 1], pool_bkv[1])
    pool_scores = jnp.einsum("he,bnhe->bhn", probe_q, pool_keys, preferred_element_type=jnp.float32) * score_scale
    local_max = jnp.max(pool_scores, axis=-1)
    pool_weights = jnp.exp(pool_scores - local_max[..., None])
    local_val = jnp.einsum("bhn,bnhe->bhe", pool_weights.astype(jnp.bfloat16), pool_vals, preferred_element_type=jnp.float32)
    return jnp.concatenate([local_max[..., None], jnp.sum(pool_weights, axis=-1)[..., None], local_val], axis=-1)


def pool_finish(gathered, pool_wout, pool_bout, pool_ln_scale, pool_ln_bias, pool_w_up, pool_b_up, pool_w_down, pool_b_down):
    group_max = jnp.max(gathered[..., 0], axis=0)
    factors = jnp.exp(gathered[..., 0] - group_max)
    total_sum = jnp.sum(factors * gathered[..., 1], axis=0)
    total_val = jnp.sum(factors[..., None] * gathered[..., 2:], axis=0)
    pooled = (total_val / total_sum[..., None]).astype(jnp.bfloat16)
    pooled_out = (jnp.einsum("bhe,hed->bd", pooled, pool_wout, preferred_element_type=jnp.float32) + pool_bout).astype(jnp.bfloat16)
    normed_out = layer_norm(pooled_out.astype(jnp.float32), pool_ln_scale, pool_ln_bias).astype(jnp.bfloat16)
    hidden_out = jax.nn.gelu(jnp.dot(normed_out, pool_w_up, preferred_element_type=jnp.float32) + pool_b_up, approximate=True).astype(jnp.bfloat16)
    return pooled_out.astype(jnp.float32) + jnp.dot(hidden_out, pool_w_down, preferred_element_type=jnp.float32) + pool_b_down


def solution(mesh):
    group_size = mesh.shape["cp"]
    send_pairs = [(source, (source + 1) % group_size) for source in range(group_size)]

    def device_step(images, ln1_scale, ln1_bias, w_qkv, b_qkv, w_out, b_out, ln2_scale, ln2_bias, w_up, b_up, w_down, b_down, lnf_scale, lnf_bias, pool_probe, pool_wq, pool_bq, pool_wkv, pool_bkv, pool_wout, pool_bout, pool_ln_scale, pool_ln_bias, pool_w_up, pool_b_up, pool_w_down, pool_b_down):
        score_scale = w_qkv.shape[-1] ** -0.5
        resid_in = images.astype(jnp.float32)
        normed = layer_norm(resid_in, ln1_scale, ln1_bias).astype(jnp.bfloat16)
        queries = project(normed, w_qkv[:, 0], b_qkv[0])
        key_rows = project(normed, w_qkv[:, 1], b_qkv[1])
        value_rows = project(normed, w_qkv[:, 2], b_qkv[2])
        attn_stats = block_stats(queries, key_rows, value_rows, score_scale)

        def visit_block(step_idx, loop_state):
            held_kv, running = loop_state
            held_kv = lax.ppermute(held_kv, "cp", send_pairs)
            running = merge_stats(running, block_stats(queries, held_kv[0], held_kv[1], score_scale))
            return held_kv, running

        attn_stats = lax.fori_loop(0, group_size - 1, visit_block, ((key_rows, value_rows), attn_stats))[1]
        context = (attn_stats[2] / attn_stats[1][..., None]).astype(jnp.bfloat16)
        tokens_out = token_tail(resid_in, context, w_out, b_out, ln2_scale, ln2_bias, w_up, b_up, w_down, b_down, lnf_scale, lnf_bias)
        local_stats = pool_stats(tokens_out, pool_probe, pool_wq, pool_bq, pool_wkv, pool_bkv, score_scale)
        gathered = lax.all_gather(local_stats, "cp")
        return pool_finish(gathered, pool_wout, pool_bout, pool_ln_scale, pool_ln_bias, pool_w_up, pool_b_up, pool_w_down, pool_b_down)

    in_specs = (P("dp", "cp", None),) + (P(),) * 27
    return jax.shard_map(device_step, mesh=mesh, in_specs=in_specs, out_specs=P("dp", None), check_vma=False)
```

profile of v0, /device:TPU:113, one launch (start us, length us, event | category | flops | bytes accessed | tf_op | source)
XLA Modules:
  0.0 718.8 jit_solution(13388415702362701137)
XLA Ops:
  10.1 6.5 add_convert_fusion.4
  20.8 5.0 add_convert_fusion.3
  35.2 593.7 %while.18 = (s32[]{:T(128)}, bf16[16,128,12,64]{1,3,2,0:T(8,128)(2,1)}, bf16[16,128,12,64]{1,3,2,0:T(8,128)(2,1)}, f32[16,12,128]{2,1,0:T(8,128)S(1)}, f32[16,12...) while((s32[]{:T(128)}, ...), condition=%wide.region_7.0_spmd, body=%wide.region_4.0_spmd.sunk | while | flops 835289088 | bytes 111476928 | solution.py:90
  38.1 34.1 %collective-permute-done = bf16[16,128,12,64]{1,3,2,0:T(8,128)(2,1)} collective-permute-done((bf16[16,128,12,64]{1,3,2,0:T(8,128)(2,1)}, bf16[16,128,12,64]{1,3,2,0:T(8,128)(2,1)}, u32[]{:S(2)}, u32[]{:S(2)}) %collective-permute-start) | collective-permute-done | bytes 3145760 | tf_op jit(solution)/shard_map/while/body/eval_jaxpr/ppermute | solution.py:86
  72.2 4.5 copy.100
  84.5 21.4 %collective-permute-done.1 = bf16[16,128,12,64]{1,3,2,0:T(8,128)(2,1)} collective-permute-done((bf16[16,128,12,64]{1,3,2,0:T(8,128)(2,1)}, bf16[16,128,12,64]{1,3,2,0:T(8,128)(2,1)}, u32[]{:S(2)}, u32[]{:S(2)}) %collective-permute-start.1) | collective-permute-done | bytes 3145760 | tf_op jit(solution)/shard_map/while/body/eval_jaxpr/ppermute | solution.py:86
  110.5 9.9 %multiply_add_fusion.5 = f32[16,12,128,64]{2,3,1,0:T(8,128)} fusion(f32[16,12,128,64]{2,3,1,0:T(8,128)} %get-tuple-element.153, f32[16,12,128]{2,1,0:T(8,128)S(1)} %get-tuple-element.138, f32[16,12,128]{2,1,0:T(8,128)S(1)} %get-tuple-element.139, bf16[16,128,12,64]{1,3,2,0:T(8,128)(2,1)} %collective-permute-done.1, ...), kind=kOutput, calls=%fused_computation.5.clone.1 | convolution fusion | flops 416808960 | bytes 28606464 | tf_op jit(solution)/shard_map/while/body/eval_jaxpr/bhqk,bkhe->bhqe/dot_general | solution.py:24
  122.8 34.2 %collective-permute-done = bf16[16,128,12,64]{1,3,2,0:T(8,128)(2,1)} collective-permute-done((bf16[16,128,12,64]{1,3,2,0:T(8,128)(2,1)}, bf16[16,128,12,64]{1,3,2,0:T(8,128)(2,1)}, u32[]{:S(2)}, u32[]{:S(2)}) %collective-permute-start) | collective-permute-done | bytes 3145760 | tf_op jit(solution)/shard_map/while/body/eval_jaxpr/ppermute | solution.py:86
  157.0 4.5 copy.100
  169.3 21.4 %collective-permute-done.1 = bf16[16,128,12,64]{1,3,2,0:T(8,128)(2,1)} collective-permute-done((bf16[16,128,12,64]{1,3,2,0:T(8,128)(2,1)}, bf16[16,128,12,64]{1,3,2,0:T(8,128)(2,1)}, u32[]{:S(2)}, u32[]{:S(2)}) %collective-permute-start.1) | collective-permute-done | bytes 3145760 | tf_op jit(solution)/shard_map/while/body/eval_jaxpr/ppermute | solution.py:86
  195.2 9.9 %multiply_add_fusion.5 = f32[16,12,128,64]{2,3,1,0:T(8,128)} fusion(f32[16,12,128,64]{2,3,1,0:T(8,128)} %get-tuple-element.153, f32[16,12,128]{2,1,0:T(8,128)S(1)} %get-tuple-element.138, f32[16,12,128]{2,1,0:T(8,128)S(1)} %get-tuple-element.139, bf16[16,128,12,64]{1,3,2,0:T(8,128)(2,1)} %collective-permute-done.1, ...), kind=kOutput, calls=%fused_computation.5.clone.1 | convolution fusion | flops 416808960 | bytes 28606464 | tf_op jit(solution)/shard_map/while/body/eval_jaxpr/bhqk,bkhe->bhqe/dot_general | solution.py:24
  207.6 34.2 %collective-permute-done = bf16[16,128,12,64]{1,3,2,0:T(8,128)(2,1)} collective-permute-done((bf16[16,128,12,64]{1,3,2,0:T(8,128)(2,1)}, bf16[16,128,12,64]{1,3,2,0:T(8,128)(2,1)}, u32[]{:S(2)}, u32[]{:S(2)}) %collective-permute-start) | collective-permute-done | bytes 3145760 | tf_op jit(solution)/shard_map/while/body/eval_jaxpr/ppermute | solution.py:86
  254.1 21.4 %collective-permute-done.1 = bf16[16,128,12,64]{1,3,2,0:T(8,128)(2,1)} collective-permute-done((bf16[16,128,12,64]{1,3,2,0:T(8,128)(2,1)}, bf16[16,128,12,64]{1,3,2,0:T(8,128)(2,1)}, u32[]{:S(2)}, u32[]{:S(2)}) %collective-permute-start.1) | collective-permute-done | bytes 3145760 | tf_op jit(solution)/shard_map/while/body/eval_jaxpr/ppermute | solution.py:86
  280.0 9.9 %multiply_add_fusion.5 = f32[16,12,128,64]{2,3,1,0:T(8,128)} fusion(f32[16,12,128,64]{2,3,1,0:T(8,128)} %get-tuple-element.153, f32[16,12,128]{2,1,0:T(8,128)S(1)} %get-tuple-element.138, f32[16,12,128]{2,1,0:T(8,128)S(1)} %get-tuple-element.139, bf16[16,128,12,64]{1,3,2,0:T(8,128)(2,1)} %collective-permute-done.1, ...), kind=kOutput, calls=%fused_computation.5.clone.1 | convolution fusion | flops 416808960 | bytes 28606464 | tf_op jit(solution)/shard_map/while/body/eval_jaxpr/bhqk,bkhe->bhqe/dot_general | solution.py:24
  292.4 34.2 %collective-permute-done = bf16[16,128,12,64]{1,3,2,0:T(8,128)(2,1)} collective-permute-done((bf16[16,128,12,64]{1,3,2,0:T(8,128)(2,1)}, bf16[16,128,12,64]{1,3,2,0:T(8,128)(2,1)}, u32[]{:S(2)}, u32[]{:S(2)}) %collective-permute-start) | collective-permute-done | bytes 3145760 | tf_op jit(solution)/shard_map/while/body/eval_jaxpr/ppermute | solution.py:86
  338.8 21.4 %collective-permute-done.1 = bf16[16,128,12,64]{1,3,2,0:T(8,128)(2,1)} collective-permute-done((bf16[16,128,12,64]{1,3,2,0:T(8,128)(2,1)}, bf16[16,128,12,64]{1,3,2,0:T(8,128)(2,1)}, u32[]{:S(2)}, u32[]{:S(2)}) %collective-permute-start.1) | collective-permute-done | bytes 3145760 | tf_op jit(solution)/shard_map/while/body/eval_jaxpr/ppermute | solution.py:86
  364.7 9.9 %multiply_add_fusion.5 = f32[16,12,128,64]{2,3,1,0:T(8,128)} fusion(f32[16,12,128,64]{2,3,1,0:T(8,128)} %get-tuple-element.153, f32[16,12,128]{2,1,0:T(8,128)S(1)} %get-tuple-element.138, f32[16,12,128]{2,1,0:T(8,128)S(1)} %get-tuple-element.139, bf16[16,128,12,64]{1,3,2,0:T(8,128)(2,1)} %collective-permute-done.1, ...), kind=kOutput, calls=%fused_computation.5.clone.1 | convolution fusion | flops 416808960 | bytes 28606464 | tf_op jit(solution)/shard_map/while/body/eval_jaxpr/bhqk,bkhe->bhqe/dot_general | solution.py:24
  377.1 34.2 %collective-permute-done = bf16[16,128,12,64]{1,3,2,0:T(8,128)(2,1)} collective-permute-done((bf16[16,128,12,64]{1,3,2,0:T(8,128)(2,1)}, bf16[16,128,12,64]{1,3,2,0:T(8,128)(2,1)}, u32[]{:S(2)}, u32[]{:S(2)}) %collective-permute-start) | collective-permute-done | bytes 3145760 | tf_op jit(solution)/shard_map/while/body/eval_jaxpr/ppermute | solution.py:86
  423.6 21.4 %collective-permute-done.1 = bf16[16,128,12,64]{1,3,2,0:T(8,128)(2,1)} collective-permute-done((bf16[16,128,12,64]{1,3,2,0:T(8,128)(2,1)}, bf16[16,128,12,64]{1,3,2,0:T(8,128)(2,1)}, u32[]{:S(2)}, u32[]{:S(2)}) %collective-permute-start.1) | collective-permute-done | bytes 3145760 | tf_op jit(solution)/shard_map/while/body/eval_jaxpr/ppermute | solution.py:86
  449.5 9.9 %multiply_add_fusion.5 = f32[16,12,128,64]{2,3,1,0:T(8,128)} fusion(f32[16,12,128,64]{2,3,1,0:T(8,128)} %get-tuple-element.153, f32[16,12,128]{2,1,0:T(8,128)S(1)} %get-tuple-element.138, f32[16,12,128]{2,1,0:T(8,128)S(1)} %get-tuple-element.139, bf16[16,128,12,64]{1,3,2,0:T(8,128)(2,1)} %collective-permute-done.1, ...), kind=kOutput, calls=%fused_computation.5.clone.1 | convolution fusion | flops 416808960 | bytes 28606464 | tf_op jit(solution)/shard_map/while/body/eval_jaxpr/bhqk,bkhe->bhqe/dot_general | solution.py:24
  461.9 34.2 %collective-permute-done = bf16[16,128,12,64]{1,3,2,0:T(8,128)(2,1)} collective-permute-done((bf16[16,128,12,64]{1,3,2,0:T(8,128)(2,1)}, bf16[16,128,12,64]{1,3,2,0:T(8,128)(2,1)}, u32[]{:S(2)}, u32[]{:S(2)}) %collective-permute-start) | collective-permute-done | bytes 3145760 | tf_op jit(solution)/shard_map/while/body/eval_jaxpr/ppermute | solution.py:86
  508.4 21.4 %collective-permute-done.1 = bf16[16,128,12,64]{1,3,2,0:T(8,128)(2,1)} collective-permute-done((bf16[16,128,12,64]{1,3,2,0:T(8,128)(2,1)}, bf16[16,128,12,64]{1,3,2,0:T(8,128)(2,1)}, u32[]{:S(2)}, u32[]{:S(2)}) %collective-permute-start.1) | collective-permute-done | bytes 3145760 | tf_op jit(solution)/shard_map/while/body/eval_jaxpr/ppermute | solution.py:86
  534.3 9.9 %multiply_add_fusion.5 = f32[16,12,128,64]{2,3,1,0:T(8,128)} fusion(f32[16,12,128,64]{2,3,1,0:T(8,128)} %get-tuple-element.153, f32[16,12,128]{2,1,0:T(8,128)S(1)} %get-tuple-element.138, f32[16,12,128]{2,1,0:T(8,128)S(1)} %get-tuple-element.139, bf16[16,128,12,64]{1,3,2,0:T(8,128)(2,1)} %collective-permute-done.1, ...), kind=kOutput, calls=%fused_computation.5.clone.1 | convolution fusion | flops 416808960 | bytes 28606464 | tf_op jit(solution)/shard_map/while/body/eval_jaxpr/bhqk,bkhe->bhqe/dot_general | solution.py:24
  546.7 34.2 %collective-permute-done = bf16[16,128,12,64]{1,3,2,0:T(8,128)(2,1)} collective-permute-done((bf16[16,128,12,64]{1,3,2,0:T(8,128)(2,1)}, bf16[16,128,12,64]{1,3,2,0:T(8,128)(2,1)}, u32[]{:S(2)}, u32[]{:S(2)}) %collective-permute-start) | collective-permute-done | bytes 3145760 | tf_op jit(solution)/shard_map/while/body/eval_jaxpr/ppermute | solution.py:86
  593.1 21.4 %collective-permute-done.1 = bf16[16,128,12,64]{1,3,2,0:T(8,128)(2,1)} collective-permute-done((bf16[16,128,12,64]{1,3,2,0:T(8,128)(2,1)}, bf16[16,128,12,64]{1,3,2,0:T(8,128)(2,1)}, u32[]{:S(2)}, u32[]{:S(2)}) %collective-permute-start.1) | collective-permute-done | bytes 3145760 | tf_op jit(solution)/shard_map/while/body/eval_jaxpr/ppermute | solution.py:86
  619.0 9.9 %multiply_add_fusion.5 = f32[16,12,128,64]{2,3,1,0:T(8,128)} fusion(f32[16,12,128,64]{2,3,1,0:T(8,128)} %get-tuple-element.153, f32[16,12,128]{2,1,0:T(8,128)S(1)} %get-tuple-element.138, f32[16,12,128]{2,1,0:T(8,128)S(1)} %get-tuple-element.139, bf16[16,128,12,64]{1,3,2,0:T(8,128)(2,1)} %collective-permute-done.1, ...), kind=kOutput, calls=%fused_computation.5.clone.1 | convolution fusion | flops 416808960 | bytes 28606464 | tf_op jit(solution)/shard_map/while/body/eval_jaxpr/bhqk,bkhe->bhqe/dot_general | solution.py:24
  629.0 6.8 convert_reduce_fusion
  638.6 27.4 %convert_reduce_fusion.2 = (f32[16,128]{1,0:T(8,128)S(1)}, bf16[16,128,768]{2,1,0:T(8,128)(2,1)}) fusion(f32[768]{0:T(1024)S(1)} %copy-done.21, bf16[3072,768]{1,0:T(8,128)(2,1)} %param.41, f32[3072]{0:T(1024)S(1)} %copy-done.17, bf16[768,3072]{1,0:T(8,128)(2,1)} %param.39, bf16[16,128,768]{2,1,0:T(8,128)(2,1)} %copy-done.4, f32[768]{0:T(1024)S(1)} %copy-done.22, ...), kind=kOutput, calls=%fused_computation.33 | convolution fusion | flops 19409139712 | bytes 15774720 | tf_op jit(solution)/shard_map/bnf,fd->bnd/dot_general | solution.py:44
  669.1 5.3 add_convert_fusion.1
  675.8 6.9 fusion.51
  683.2 26.9 %all-gather = f32[128,12,66]{2,0,1:T(8,128)S(1)} all-gather(f32[16,12,66]{2,0,1:T(8,128)S(1)} %pad_maximum_fusion), channel_id=2, replica_groups=mesh['dp'=2,'cp'=8] {'cp'}, dimensions={0}, use_global_device_ids=true | all-gather | bytes 456192 | tf_op jit(solution)/shard_map/all_gather | solution.py:94
  712.4 5.9 fusion.91
  (145 shorter events, 159.7 us)
Async XLA Ops:
  0.0 628.9 %copy-start = (bf16[12,64,768]{2,1,0:T(8,128)(2,1)S(1)}, bf16[12,64,768]{2,1,0:T(8,128)(2,1)}, u32[]{:S(2)}) copy-start(bf16[12,64,768]{2,1,0:T(8,128)(2,1)} %param.35) | copy-start | bytes 3538948
  35.2 593.8 %copy-start.20 = (f32[768]{0:T(1024)S(1)}, f32[768]{0:T(1024)}, u32[]{:S(2)}) copy-start(f32[768]{0:T(1024)} %param.36) | copy-start | bytes 9220
  35.4 36.9 %collective-permute-start = (bf16[16,128,12,64]{1,3,2,0:T(8,128)(2,1)}, bf16[16,128,12,64]{1,3,2,0:T(8,128)(2,1)}, u32[]{:S(2)}, u32[]{:S(2)}) collective-permute-start(bf16[16,128,12,64]{1,3,2,0:T(8,128)(2,1)} %get-tuple-element.149), channel_id=1, source_target_pairs={{0,1},{1,2},{2,3},{3,4},{4,5},{5,6},{6,7},{7,0},{8,9},{9,10},{10,1... | collective-permute-start | bytes 9437192 | tf_op jit(solution)/shard_map/while/body/eval_jaxpr/ppermute | solution.py:86
  38.1 67.9 %collective-permute-start.1 = (bf16[16,128,12,64]{1,3,2,0:T(8,128)(2,1)}, bf16[16,128,12,64]{1,3,2,0:T(8,128)(2,1)}, u32[]{:S(2)}, u32[]{:S(2)}) collective-permute-start(bf16[16,128,12,64]{1,3,2,0:T(8,128)(2,1)} %get-tuple-element.150), channel_id=1, source_target_pairs={{0,1},{1,2},{2,3},{3,4},{4,5},{5,6},{6,7},{7,0},{8,9},{9,10},{10,1... | collective-permute-start | bytes 9437192 | tf_op jit(solution)/shard_map/while/body/eval_jaxpr/ppermute | solution.py:86
  38.1 38.6 %copy-start.2 = (bf16[16,128,12,64]{1,3,2,0:T(8,128)(2,1)S(1)}, bf16[16,128,12,64]{1,3,2,0:T(8,128)(2,1)}, u32[]{:S(2)}) copy-start(bf16[16,128,12,64]{1,3,2,0:T(8,128)(2,1)} %get-tuple-element.162) | copy-start | bytes 9437188 | tf_op jit(solution)/shard_map/while
  120.3 36.7 %collective-permute-start = (bf16[16,128,12,64]{1,3,2,0:T(8,128)(2,1)}, bf16[16,128,12,64]{1,3,2,0:T(8,128)(2,1)}, u32[]{:S(2)}, u32[]{:S(2)}) collective-permute-start(bf16[16,128,12,64]{1,3,2,0:T(8,128)(2,1)} %get-tuple-element.149), channel_id=1, source_target_pairs={{0,1},{1,2},{2,3},{3,4},{4,5},{5,6},{6,7},{7,0},{8,9},{9,10},{10,1... | collective-permute-start | bytes 9437192 | tf_op jit(solution)/shard_map/while/body/eval_jaxpr/ppermute | solution.py:86
  122.8 67.9 %collective-permute-start.1 = (bf16[16,128,12,64]{1,3,2,0:T(8,128)(2,1)}, bf16[16,128,12,64]{1,3,2,0:T(8,128)(2,1)}, u32[]{:S(2)}, u32[]{:S(2)}) collective-permute-start(bf16[16,128,12,64]{1,3,2,0:T(8,128)(2,1)} %get-tuple-element.150), channel_id=1, source_target_pairs={{0,1},{1,2},{2,3},{3,4},{4,5},{5,6},{6,7},{7,0},{8,9},{9,10},{10,1... | collective-permute-start | bytes 9437192 | tf_op jit(solution)/shard_map/while/body/eval_jaxpr/ppermute | solution.py:86
  122.8 38.7 %copy-start.2 = (bf16[16,128,12,64]{1,3,2,0:T(8,128)(2,1)S(1)}, bf16[16,128,12,64]{1,3,2,0:T(8,128)(2,1)}, u32[]{:S(2)}) copy-start(bf16[16,128,12,64]{1,3,2,0:T(8,128)(2,1)} %get-tuple-element.162) | copy-start | bytes 9437188 | tf_op jit(solution)/shard_map/while
  205.1 36.7 %collective-permute-start = (bf16[16,128,12,64]{1,3,2,0:T(8,128)(2,1)}, bf16[16,128,12,64]{1,3,2,0:T(8,128)(2,1)}, u32[]{:S(2)}, u32[]{:S(2)}) collective-permute-start(bf16[16,128,12,64]{1,3,2,0:T(8,128)(2,1)} %get-tuple-element.149), channel_id=1, source_target_pairs={{0,1},{1,2},{2,3},{3,4},{4,5},{5,6},{6,7},{7,0},{8,9},{9,10},{10,1... | collective-permute-start | bytes 9437192 | tf_op jit(solution)/shard_map/while/body/eval_jaxpr/ppermute | solution.py:86
  207.6 67.9 %collective-permute-start.1 = (bf16[16,128,12,64]{1,3,2,0:T(8,128)(2,1)}, bf16[16,128,12,64]{1,3,2,0:T(8,128)(2,1)}, u32[]{:S(2)}, u32[]{:S(2)}) collective-permute-start(bf16[16,128,12,64]{1,3,2,0:T(8,128)(2,1)} %get-tuple-element.150), channel_id=1, source_target_pairs={{0,1},{1,2},{2,3},{3,4},{4,5},{5,6},{6,7},{7,0},{8,9},{9,10},{10,1... | collective-permute-start | bytes 9437192 | tf_op jit(solution)/shard_map/while/body/eval_jaxpr/ppermute | solution.py:86
  207.6 38.7 %copy-start.2 = (bf16[16,128,12,64]{1,3,2,0:T(8,128)(2,1)S(1)}, bf16[16,128,12,64]{1,3,2,0:T(8,128)(2,1)}, u32[]{:S(2)}) copy-start(bf16[16,128,12,64]{1,3,2,0:T(8,128)(2,1)} %get-tuple-element.162) | copy-start | bytes 9437188 | tf_op jit(solution)/shard_map/while
  289.8 36.7 %collective-permute-start = (bf16[16,128,12,64]{1,3,2,0:T(8,128)(2,1)}, bf16[16,128,12,64]{1,3,2,0:T(8,128)(2,1)}, u32[]{:S(2)}, u32[]{:S(2)}) collective-permute-start(bf16[16,128,12,64]{1,3,2,0:T(8,128)(2,1)} %get-tuple-element.149), channel_id=1, source_target_pairs={{0,1},{1,2},{2,3},{3,4},{4,5},{5,6},{6,7},{7,0},{8,9},{9,10},{10,1... | collective-permute-start | bytes 9437192 | tf_op jit(solution)/shard_map/while/body/eval_jaxpr/ppermute | solution.py:86
  292.3 67.9 %collective-permute-start.1 = (bf16[16,128,12,64]{1,3,2,0:T(8,128)(2,1)}, bf16[16,128,12,64]{1,3,2,0:T(8,128)(2,1)}, u32[]{:S(2)}, u32[]{:S(2)}) collective-permute-start(bf16[16,128,12,64]{1,3,2,0:T(8,128)(2,1)} %get-tuple-element.150), channel_id=1, source_target_pairs={{0,1},{1,2},{2,3},{3,4},{4,5},{5,6},{6,7},{7,0},{8,9},{9,10},{10,1... | collective-permute-start | bytes 9437192 | tf_op jit(solution)/shard_map/while/body/eval_jaxpr/ppermute | solution.py:86
  292.4 38.7 %copy-start.2 = (bf16[16,128,12,64]{1,3,2,0:T(8,128)(2,1)S(1)}, bf16[16,128,12,64]{1,3,2,0:T(8,128)(2,1)}, u32[]{:S(2)}) copy-start(bf16[16,128,12,64]{1,3,2,0:T(8,128)(2,1)} %get-tuple-element.162) | copy-start | bytes 9437188 | tf_op jit(solution)/shard_map/while
  374.6 36.7 %collective-permute-start = (bf16[16,128,12,64]{1,3,2,0:T(8,128)(2,1)}, bf16[16,128,12,64]{1,3,2,0:T(8,128)(2,1)}, u32[]{:S(2)}, u32[]{:S(2)}) collective-permute-start(bf16[16,128,12,64]{1,3,2,0:T(8,128)(2,1)} %get-tuple-element.149), channel_id=1, source_target_pairs={{0,1},{1,2},{2,3},{3,4},{4,5},{5,6},{6,7},{7,0},{8,9},{9,10},{10,1... | collective-permute-start | bytes 9437192 | tf_op jit(solution)/shard_map/while/body/eval_jaxpr/ppermute | solution.py:86
  377.1 67.9 %collective-permute-start.1 = (bf16[16,128,12,64]{1,3,2,0:T(8,128)(2,1)}, bf16[16,128,12,64]{1,3,2,0:T(8,128)(2,1)}, u32[]{:S(2)}, u32[]{:S(2)}) collective-permute-start(bf16[16,128,12,64]{1,3,2,0:T(8,128)(2,1)} %get-tuple-element.150), channel_id=1, source_target_pairs={{0,1},{1,2},{2,3},{3,4},{4,5},{5,6},{6,7},{7,0},{8,9},{9,10},{10,1... | collective-permute-start | bytes 9437192 | tf_op jit(solution)/shard_map/while/body/eval_jaxpr/ppermute | solution.py:86
  377.1 38.7 %copy-start.2 = (bf16[16,128,12,64]{1,3,2,0:T(8,128)(2,1)S(1)}, bf16[16,128,12,64]{1,3,2,0:T(8,128)(2,1)}, u32[]{:S(2)}) copy-start(bf16[16,128,12,64]{1,3,2,0:T(8,128)(2,1)} %get-tuple-element.162) | copy-start | bytes 9437188 | tf_op jit(solution)/shard_map/while
  459.4 36.7 %collective-permute-start = (bf16[16,128,12,64]{1,3,2,0:T(8,128)(2,1)}, bf16[16,128,12,64]{1,3,2,0:T(8,128)(2,1)}, u32[]{:S(2)}, u32[]{:S(2)}) collective-permute-start(bf16[16,128,12,64]{1,3,2,0:T(8,128)(2,1)} %get-tuple-element.149), channel_id=1, source_target_pairs={{0,1},{1,2},{2,3},{3,4},{4,5},{5,6},{6,7},{7,0},{8,9},{9,10},{10,1... | collective-permute-start | bytes 9437192 | tf_op jit(solution)/shard_map/while/body/eval_jaxpr/ppermute | solution.py:86
  461.9 67.9 %collective-permute-start.1 = (bf16[16,128,12,64]{1,3,2,0:T(8,128)(2,1)}, bf16[16,128,12,64]{1,3,2,0:T(8,128)(2,1)}, u32[]{:S(2)}, u32[]{:S(2)}) collective-permute-start(bf16[16,128,12,64]{1,3,2,0:T(8,128)(2,1)} %get-tuple-element.150), channel_id=1, source_target_pairs={{0,1},{1,2},{2,3},{3,4},{4,5},{5,6},{6,7},{7,0},{8,9},{9,10},{10,1... | collective-permute-start | bytes 9437192 | tf_op jit(solution)/shard_map/while/body/eval_jaxpr/ppermute | solution.py:86
  461.9 38.7 %copy-start.2 = (bf16[16,128,12,64]{1,3,2,0:T(8,128)(2,1)S(1)}, bf16[16,128,12,64]{1,3,2,0:T(8,128)(2,1)}, u32[]{:S(2)}) copy-start(bf16[16,128,12,64]{1,3,2,0:T(8,128)(2,1)} %get-tuple-element.162) | copy-start | bytes 9437188 | tf_op jit(solution)/shard_map/while
  544.1 36.7 %collective-permute-start = (bf16[16,128,12,64]{1,3,2,0:T(8,128)(2,1)}, bf16[16,128,12,64]{1,3,2,0:T(8,128)(2,1)}, u32[]{:S(2)}, u32[]{:S(2)}) collective-permute-start(bf16[16,128,12,64]{1,3,2,0:T(8,128)(2,1)} %get-tuple-element.149), channel_id=1, source_target_pairs={{0,1},{1,2},{2,3},{3,4},{4,5},{5,6},{6,7},{7,0},{8,9},{9,10},{10,1... | collective-permute-start | bytes 9437192 | tf_op jit(solution)/shard_map/while/body/eval_jaxpr/ppermute | solution.py:86
  546.6 67.9 %collective-permute-start.1 = (bf16[16,128,12,64]{1,3,2,0:T(8,128)(2,1)}, bf16[16,128,12,64]{1,3,2,0:T(8,128)(2,1)}, u32[]{:S(2)}, u32[]{:S(2)}) collective-permute-start(bf16[16,128,12,64]{1,3,2,0:T(8,128)(2,1)} %get-tuple-element.150), channel_id=1, source_target_pairs={{0,1},{1,2},{2,3},{3,4},{4,5},{5,6},{6,7},{7,0},{8,9},{9,10},{10,1... | collective-permute-start | bytes 9437192 | tf_op jit(solution)/shard_map/while/body/eval_jaxpr/ppermute | solution.py:86
  546.7 38.7 %copy-start.2 = (bf16[16,128,12,64]{1,3,2,0:T(8,128)(2,1)S(1)}, bf16[16,128,12,64]{1,3,2,0:T(8,128)(2,1)}, u32[]{:S(2)}) copy-start(bf16[16,128,12,64]{1,3,2,0:T(8,128)(2,1)} %get-tuple-element.162) | copy-start | bytes 9437188 | tf_op jit(solution)/shard_map/while
  638.5 30.4 %copy-start.10 = (f32[2,12,64]{2,0,1:T(2,128)S(1)}, f32[2,12,64]{2,0,1:T(2,128)}, u32[]{:S(2)}) copy-start(f32[2,12,64]{2,0,1:T(2,128)} %param.49) | copy-start | bytes 18436
  638.6 30.5 %copy-start.24 = (f32[768]{0:T(1024)S(1)}, f32[768]{0:T(1024)}, u32[]{:S(2)}) copy-start(f32[768]{0:T(1024)} %param.44) | copy-start | bytes 9220
  638.6 30.5 %copy-start.25 = (f32[768]{0:T(1024)S(1)}, f32[768]{0:T(1024)}, u32[]{:S(2)}) copy-start(f32[768]{0:T(1024)} %param.43) | copy-start | bytes 9220
  675.8 35.8 %copy-start.6 = (bf16[12,64,768]{2,1,0:T(8,128)(2,1)S(1)}, bf16[12,64,768]{2,1,0:T(8,128)(2,1)}, u32[]{:S(2)}) copy-start(bf16[12,64,768]{2,1,0:T(8,128)(2,1)} %param.50) | copy-start | bytes 3538948
  675.8 35.8 %copy-start.12 = (f32[768]{0:T(1024)S(1)}, f32[768]{0:T(1024)}, u32[]{:S(2)}) copy-start(f32[768]{0:T(1024)} %param.51) | copy-start | bytes 9220
  682.7 29.7 %copy-start.9 = (f32[3072]{0:T(1024)S(1)}, f32[3072]{0:T(1024)}, u32[]{:S(2)}) copy-start(f32[3072]{0:T(1024)} %param.55) | copy-start | bytes 36868
  682.7 29.7 %copy-start.13 = (f32[768]{0:T(1024)S(1)}, f32[768]{0:T(1024)}, u32[]{:S(2)}) copy-start(f32[768]{0:T(1024)} %param.57) | copy-start | bytes 9220
  682.7 29.7 %copy-start.14 = (f32[768]{0:T(1024)S(1)}, f32[768]{0:T(1024)}, u32[]{:S(2)}) copy-start(f32[768]{0:T(1024)} %param.53) | copy-start | bytes 9220
  682.7 29.7 %copy-start.15 = (f32[768]{0:T(1024)S(1)}, f32[768]{0:T(1024)}, u32[]{:S(2)}) copy-start(f32[768]{0:T(1024)} %param.52) | copy-start | bytes 9220
  (14 other events, 87.1 us)
where the time goes:
time: 732 us; the launch traced here: 719 us
  waiting for transfers between devices  389 us (53%)
  matrix products  176 us (24%)
  local copies, waits for them, and re-layouts  66.8 us (9%)
  other arithmetic  40.7 us (6%)
  blocking collectives  26.9 us (4%)
  starting transfers between devices  17.9 us (2%)
    ppermute x14, waiting for transfers between devices, visit_block(): held_kv = lax.ppermute(held_kv, 'cp', send_pairs)  389 us
    dot_general x8, matrix products, block_stats(): jnp.einsum('bhqk,bkhe->bhqe', weights.astype(jnp.bfloat16), value_rows, p...  72.9 us
    while x28, local copies, waits for them, and re-layouts  63 us
    dot_general x8, matrix products, block_stats(): jnp.einsum('bqhe,bkhe->bhqk', queries, key_rows, preferred_element_type=j...  33.3 us
    reduce_sum x8, other arithmetic, block_stats(): return (row_max, jnp.sum(weights, axis=-1), value_sum)  28.2 us
    dot_general x1, matrix products, token_tail(): jnp.einsum('bnf,fd->bnd', hidden, w_down, preferred_element_type=jnp.floa...  27.4 us
    all_gather x1, blocking collectives, device_step(): gathered = lax.all_gather(local_stats, 'cp')  26.9 us
    dot_general x4, matrix products, project(): jnp.einsum('bnd,dhe->bnhe', normed, weight, preferred_element_type=jnp.fl...  21.3 us
  transfers between devices with their start and end apart: 14, of which 14 were waited for; matrix products, arithmetic and copies ran while one was open for 12% of the time, Pallas kernels for 0%

commit v1 on v0

v1 whole, which is shorter than its diff:
```python
import functools
import math

import jax
import jax.numpy as jnp
from jax import lax
from jax.experimental import pallas as pl
from jax.experimental.pallas import tpu as pltpu
from jax.sharding import PartitionSpec as P

EPSILON = 1e-6
LANES = 128
BLOCK = 256
F32 = jnp.float32
BF16 = jnp.bfloat16

(LN1_G, LN1_B, B_OUT, LN2_G, LN2_B, B_DOWN, LNF_G, LNF_B, P_BOUT, P_LN_G, P_LN_B, P_BDOWN, B_Q, B_K, B_V, P_BQ, P_BK, P_BV) = range(18)
N_FIXED = 18
N_SMALL = 17


def layer_norm(values, ln_gain, ln_shift):
    row_mean = jnp.mean(values, axis=-1, keepdims=True)
    centered = values - row_mean
    variance = jnp.mean(centered * centered, axis=-1, keepdims=True)
    return centered * lax.rsqrt(variance + EPSILON) * ln_gain + ln_shift


def gelu(x):
    return jax.nn.gelu(x, approximate=True)


def dot(a, b):
    return lax.dot_general(a, b, (((1,), (0,)), ((), ())), preferred_element_type=F32)


def dot_t(a, b):
    return lax.dot_general(a, b, (((1,), (1,)), ((), ())), preferred_element_type=F32)


def kernel(cfg, images, wqkv_h, wout_h, wup_h, wdown_h, wpkv_h, wpq_h, pwout_h, pwup_h, pwdown_h, *rest):
    n, per, heads, head_dim, width, mlp = cfg
    smalls = rest[:N_SMALL]
    (probe_h, out_ref,
           wqkv, wout, wup, wdown, wpkv, wpq, pwout, pwup, pwdown,
           xbuf, qz, kbuf, vt, s00, s01, s10, s11, p00, p01, p10, p11, mbuf, ctx, hbuf, rbuf, nbuf, hid, zbuf,
           score, pvbuf, ubuf, cols, abuf, gath, vecs, probe, *tail_refs) = rest[N_SMALL:]
    small_bufs = tail_refs[:N_SMALL]
    send_sem, recv_sem, w_sem, gsend_sem, grecv_sem, v_sem = tail_refs[N_SMALL:]
    run = images.shape[1]
    tokens = n * run
    nch = n // 2
    hid_chunks = mlp // width
    pairs = heads // 2
    nq = tokens // BLOCK
    nsteps = pairs * nq
    exp_scale = math.log2(math.e) * head_dim ** -0.5
    me = lax.axis_index("cp")
    own = me // 2
    core = me % 2

    def vec(i):
        return vecs[i:i + 1, :]

    def weight_copy(i, src, dst):
        return pltpu.make_async_copy(src, dst, w_sem.at[i])

    weights = [(wqkv_h, wqkv), (wout_h, wout), (wpq_h, wpq), (wup_h, wup), (wdown_h, wdown), (wpkv_h, wpkv), (pwout_h, pwout), (pwup_h, pwup), (pwdown_h, pwdown)]

    def start_weight(i):
        weight_copy(i, *weights[i]).start()

    def wait_weight(i):
        weight_copy(i, *weights[i]).wait()

    def local_copy(j):
        return pltpu.make_async_copy(images.at[me * per + j], xbuf.at[j, me], recv_sem.at[j, me])

    deltas = [0]
    for d in range(1, nch // 2 + 1):
        deltas.append(d)
        if nch - d != d:
            deltas.append(nch - d)

    def sends(j):
        copies = []
        for delta in deltas:
            for cc in (0, 1):
                if delta == 0 and cc == 0:
                    continue
                dst = ((own + delta) % nch) * 2 + (core + cc) % 2
                copies.append(pltpu.make_async_remote_copy(
                    src_ref=images.at[dst * per + j],
                    dst_ref=xbuf.at[j, me],
                    send_sem=send_sem.at[j, len(copies)],
                    recv_sem=recv_sem.at[j, me],
                    device_id={"cp": dst},
                    device_id_type=pl.DeviceIdType.MESH,
                ))
        return copies

    small_copies = [pltpu.make_async_copy(src, dst, v_sem.at[i]) for i, (src, dst) in enumerate(zip((*smalls, probe_h), (*small_bufs, probe)))]
    start_weight(0)
    for j in range(per):
        local_copy(j).start()
    for copy in small_copies:
        copy.start()

    barrier = pltpu.get_barrier_semaphore()
    for s in range(1, n):
        pl.semaphore_signal(barrier, inc=1, device_id={"cp": (me + s) % n}, device_id_type=pl.DeviceIdType.MESH)
    pl.semaphore_wait(barrier, n - 1)

    for j in range(per):
        for copy in sends(j):
            copy.start()
    for i in range(1, len(weights)):
        start_weight(i)

    for copy in small_copies:
        copy.wait()
    for i, buf in enumerate(small_bufs[:12]):
        vecs[i:i + 1, :] = buf[...].reshape(1, width)
    bqkv_b, pbq_b, pbkv_b, bup_b, pbup_b = small_bufs[12:]
    for h in range(heads):
        lanes = slice(h * head_dim, (h + 1) * head_dim)
        for i, row in enumerate((B_Q, B_K, B_V)):
            vecs[row:row + 1, lanes] = bqkv_b[i, h:h + 1, :]
        vecs[P_BQ:P_BQ + 1, lanes] = pbq_b[h:h + 1, :]
        for i, row in enumerate((P_BK, P_BV)):
            vecs[row:row + 1, lanes] = pbkv_b[h, i:i + 1, :]
    for hc in range(hid_chunks):
        span = slice(hc * width, (hc + 1) * width)
        vecs[N_FIXED + hc:N_FIXED + hc + 1, :] = bup_b[span].reshape(1, width)
        vecs[N_FIXED + hid_chunks + hc:N_FIXED + hid_chunks + hc + 1, :] = pbup_b[span].reshape(1, width)
    for slot, row in enumerate((B_Q, B_V, P_BK)):
        cols[slot] = jnp.transpose(jnp.broadcast_to(vec(row), (LANES, width)))
    qz[...] = jnp.zeros_like(qz)
    abuf[...] = jnp.zeros_like(abuf)
    wait_weight(0)

    def col_bias(slot, lo, size):
        tile = cols[slot, lo:lo + size, :]
        return jnp.concatenate([tile] * (BLOCK // LANES), axis=1)

    def wait_source(j, src):
        pltpu.make_async_copy(images.at[0], xbuf.at[j, src], recv_sem.at[j, src]).wait()

    s_refs = ((s00, s01), (s10, s11))
    p_refs = ((p00, p01), (p10, p11))

    def one_image(j, carry):
        for delta in deltas:
            chip = (own + delta) % nch
            wait_source(j, chip * 2)
            wait_source(j, chip * 2 + 1)
            tok = pl.multiple_of(chip * BLOCK, BLOCK)
            x = xbuf[j, pl.ds(chip * 2, 2)].reshape(BLOCK, width)
            for r0 in range(0, BLOCK, 64):
                hbuf[r0:r0 + 64, :] = layer_norm(x[r0:r0 + 64].astype(F32), vec(LN1_G), vec(LN1_B)).astype(BF16)
            h = hbuf[...]
            kbuf[pl.ds(tok, BLOCK), :] = (dot_t(h, wqkv[width:2 * width, :]) + vec(B_K)).astype(BF16)
            qt = (dot_t(wqkv[0:width, :], h) + col_bias(0, 0, width)).astype(BF16)
            for hd in range(heads):
                off = (hd % 2) * head_dim
                qz[hd, off:off + head_dim, pl.ds(tok, BLOCK)] = qt[hd * head_dim:(hd + 1) * head_dim]
            vt[:, pl.ds(tok, BLOCK)] = (dot_t(wqkv[2 * width:3 * width, :], h) + col_bias(1, 0, width)).astype(BF16)

        def qk(step, slot):
            hp, qb = step // nq, step % nq
            keys = kbuf[:, pl.ds(pl.multiple_of(hp * LANES, LANES), LANES)]
            for hh in (0, 1):
                q = qz[hp * 2 + hh, :, pl.ds(pl.multiple_of(qb * BLOCK, BLOCK), BLOCK)]
                s = dot(keys, q)
                s_refs[slot][hh][...] = s
                mbuf[slot, hh] = jnp.max(s.reshape(tokens // 8, 8, BLOCK), axis=0)

        def softmax_pv(step, slot):
            hp, qb = step // nq, step % nq
            outs = []
            for hh in (0, 1):
                s_ref, p_ref = s_refs[slot][hh], p_refs[slot][hh]
                m = jnp.max(mbuf[slot, hh], axis=0, keepdims=True)
                total = jnp.zeros((8, BLOCK), F32)
                for kc in range(0, tokens, LANES):
                    p = jnp.exp2((s_ref[kc:kc + LANES, :] - m) * exp_scale)
                    total = total + jnp.sum(p.reshape(LANES // 8, 8, BLOCK), axis=0)
                    p_ref[kc:kc + LANES, :] = p.astype(BF16)
                row_sum = jnp.sum(total, axis=0, keepdims=True)
                v = vt[pl.ds(pl.multiple_of(hp * LANES + hh * head_dim, head_dim), head_dim), :]
                outs.append(dot(v, p_ref[...]) * (1.0 / row_sum))
            pair = jnp.transpose(jnp.concatenate(outs, axis=0)).astype(BF16)
            ctx[pl.ds(pl.multiple_of(qb * BLOCK, BLOCK), BLOCK), pl.ds(pl.multiple_of(hp * LANES, LANES), LANES)] = pair

        qk(0, 0)

        def attend(i, c):
            qk(2 * i + 1, 1)
            softmax_pv(2 * i, 0)
            qk((2 * i + 2) % nsteps, 0)
            softmax_pv(2 * i + 1, 1)
            return c

        lax.fori_loop(0, nsteps // 2, attend, 0)

        @pl.when(j == 0)
        def _():
            for i in range(1, 6):
                wait_weight(i)
            q16 = jnp.broadcast_to(probe[...], (16, width))
            u = dot_t(q16, wpq[...]) + vec(P_BQ)
            row = lax.broadcasted_iota(jnp.int32, (16, width), 0)
            col = lax.broadcasted_iota(jnp.int32, (16, width), 1)
            ubuf[...] = jnp.where(col // head_dim == row, u, 0.0).astype(BF16)

        def tail(i, c):
            starts = [pl.multiple_of((2 * i + t) * BLOCK, BLOCK) for t in (0, 1)]

            def resid(t):
                chip = 2 * i + t
                x = xbuf[j, pl.ds(chip * 2, 2)].reshape(BLOCK, width)
                a = dot(ctx[pl.ds(starts[t], BLOCK), :], wout[...])
                rbuf[t] = (x.astype(F32) + a + vec(B_OUT)).astype(BF16)

            def norm(t):
                for r0 in range(0, BLOCK, 64):
                    nbuf[t, r0:r0 + 64, :] = layer_norm(rbuf[t, r0:r0 + 64, :].astype(F32), vec(LN2_G), vec(LN2_B)).astype(BF16)

            def up(t):
                for hc in range(hid_chunks):
                    cols_ = slice(hc * width, (hc + 1) * width)
                    hid[t, :, cols_] = gelu(dot(nbuf[t], wup[:, cols_]) + vec(N_FIXED + hc)).astype(BF16)

            def down(t):
                y = (rbuf[t].astype(F32) + dot(hid[t], wdown[...]) + vec(B_DOWN)).astype(BF16)
                for r0 in range(0, BLOCK, 64):
                    zbuf[t, r0:r0 + 64, :] = layer_norm(y[r0:r0 + 64].astype(F32), vec(LNF_G), vec(LNF_B)).astype(BF16)

            def pool(t):
                z = zbuf[t]
                pk = (dot_t(wpkv[0:width, :], z) + col_bias(2, 0, width)).astype(BF16)
                score[:, pl.ds(starts[t], BLOCK)] = dot(ubuf[...], pk)
                pvbuf[pl.ds(starts[t], BLOCK), :] = (dot_t(z, wpkv[width:2 * width, :]) + vec(P_BV)).astype(BF16)

            resid(0)
            resid(1)
            norm(0)
            up(0)
            norm(1)
            down(0)
            up(1)
            pool(0)
            down(1)
            pool(1)
            return c

        lax.fori_loop(0, nq // 2, tail, 0)

        s = score[...]
        w = jnp.exp2((s - jnp.max(s, axis=-1, keepdims=True)) * exp_scale)
        a = dot(w.astype(BF16), pvbuf[...]) / jnp.sum(w, axis=-1, keepdims=True)
        row = lax.broadcasted_iota(jnp.int32, (16, width), 0)
        col = lax.broadcasted_iota(jnp.int32, (16, width), 1)
        abuf[pl.ds(j, 1), :] = jnp.sum(jnp.where(col // head_dim == row, a, 0.0), axis=0, keepdims=True)
        return carry

    lax.fori_loop(0, per, one_image, 0)

    for i in range(6, len(weights)):
        wait_weight(i)
    o = (dot(abuf[...].astype(BF16), pwout[...]) + vec(P_BOUT)).astype(BF16).astype(F32)
    normed = layer_norm(o, vec(P_LN_G), vec(P_LN_B)).astype(BF16)
    emb = o + vec(P_BDOWN)
    for hc in range(hid_chunks):
        cols_ = slice(hc * width, (hc + 1) * width)
        m = gelu(dot(normed, pwup[:, cols_]) + vec(N_FIXED + hid_chunks + hc)).astype(BF16)
        emb = emb + dot(m, pwdown[cols_, :])
    gath[pl.ds(me, 1)] = emb[0:8][None]

    copies = []
    for s in range(1, n):
        copies.append(pltpu.make_async_remote_copy(
            src_ref=gath.at[me],
            dst_ref=gath.at[me],
            send_sem=gsend_sem.at[s],
            recv_sem=grecv_sem.at[me],
            device_id={"cp": (me + s) % n},
            device_id_type=pl.DeviceIdType.MESH,
        ))
    for copy in copies:
        copy.start()
    for j in range(per):
        for copy in sends(j):
            copy.wait_send()
    for s in range(1, n):
        src = (me + s) % n
        pltpu.make_async_remote_copy(
            src_ref=gath.at[src], dst_ref=gath.at[src], send_sem=gsend_sem.at[s], recv_sem=grecv_sem.at[src],
            device_id={"cp": src}, device_id_type=pl.DeviceIdType.MESH,
        ).wait_recv()
    for copy in copies:
        copy.wait_send()
    for s in range(n):
        out_ref[s * per:(s + 1) * per, :] = gath[s, 0:per, :]


def solution(mesh):
    n = mesh.shape["cp"]

    def device_step(images, ln1_scale, ln1_bias, w_qkv, b_qkv, w_out, b_out, ln2_scale, ln2_bias, w_up, b_up, w_down, b_down, lnf_scale, lnf_bias, pool_probe, pool_wq, pool_bq, pool_wkv, pool_bkv, pool_wout, pool_bout, pool_ln_scale, pool_ln_bias, pool_w_up, pool_b_up, pool_w_down, pool_b_down):
        count, run, width = images.shape
        heads, head_dim = w_qkv.shape[2:]
        mlp = w_up.shape[1]
        per = count // n
        tokens = n * run
        wqkv_t = jnp.transpose(w_qkv, (1, 2, 3, 0)).reshape(3 * width, width)
        wpkv_t = jnp.transpose(pool_wkv, (1, 2, 3, 0)).reshape(2 * width, width)
        wpq_t = jnp.transpose(pool_wq, (1, 2, 0)).reshape(width, width)
        wout2 = w_out.reshape(width, width)
        pwout2 = pool_wout.reshape(width, width)
        smalls = (ln1_scale, ln1_bias, b_out, ln2_scale, ln2_bias, b_down, lnf_scale, lnf_bias, pool_bout, pool_ln_scale, pool_ln_bias, pool_b_down, b_qkv, pool_bq, jnp.transpose(pool_bkv, (1, 0, 2)), b_up, pool_b_up)
        any_spec = pl.BlockSpec(memory_space=pl.ANY)
        vmem_spec = pl.BlockSpec(memory_space=pltpu.VMEM)
        big = (images, wqkv_t, wout2, w_up, w_down, wpkv_t, wpq_t, pwout2, pool_w_up, pool_w_down)
        scratch = [pltpu.VMEM(w.shape, BF16) for w in big[1:]] + [
            pltpu.VMEM((per, n, run, width), BF16),
            pltpu.VMEM((heads, LANES, tokens), BF16),
            pltpu.VMEM((tokens, width), BF16),
            pltpu.VMEM((width, tokens), BF16),
            *[pltpu.VMEM((tokens, BLOCK), F32) for _ in range(4)],
            *[pltpu.VMEM((tokens, BLOCK), BF16) for _ in range(4)],
            pltpu.VMEM((2, 2, 8, BLOCK), F32),
            pltpu.VMEM((tokens, width), BF16),
            pltpu.VMEM((BLOCK, width), BF16),
            pltpu.VMEM((2, BLOCK, width), BF16),
            pltpu.VMEM((2, BLOCK, width), BF16),
            pltpu.VMEM((2, BLOCK, mlp), BF16),
            pltpu.VMEM((2, BLOCK, width), BF16),
            pltpu.VMEM((16, tokens), F32),
            pltpu.VMEM((tokens, width), BF16),
            pltpu.VMEM((16, width), BF16),
            pltpu.VMEM((3, width, LANES), F32),
            pltpu.VMEM((16, width), F32),
            pltpu.VMEM((n, 8, width), F32),
            pltpu.VMEM((N_FIXED + 2 * mlp // width, width), F32),
            pltpu.VMEM(pool_probe.shape, BF16),
            *[pltpu.VMEM(v.shape, F32) for v in smalls],
            pltpu.SemaphoreType.DMA((per, n)),
            pltpu.SemaphoreType.DMA((per, n)),
            pltpu.SemaphoreType.DMA((len(big) - 1,)),
            pltpu.SemaphoreType.DMA((n,)),
            pltpu.SemaphoreType.DMA((n,)),
            pltpu.SemaphoreType.DMA((N_SMALL + 1,)),
        ]
        return pl.pallas_call(
            functools.partial(kernel, (n, per, heads, head_dim, width, mlp)),
            out_shape=jax.ShapeDtypeStruct((count, width), F32),
            in_specs=[any_spec] * (len(big) + len(smalls) + 1),
            out_specs=vmem_spec,
            scratch_shapes=scratch,
            compiler_params=pltpu.CompilerParams(collective_id=0, has_side_effects=True, vmem_limit_bytes=67043328),
            name="encoder_pool",
        )(*big, *smalls, pool_probe)

    in_specs = (P("dp", "cp", None),) + (P(),) * 27
    return jax.shard_map(device_step, mesh=mesh, in_specs=in_specs, out_specs=P("dp", None), check_vma=False)
```

time: 732 us -> 109 us (0.15); the launches traced: 719 us -> 109 us
  waiting for transfers between devices: 389 us -> 0 us
  matrix products: 176 us -> 0 us
  Pallas kernels: 0 us -> 108 us
  local copies, waits for them, and re-layouts: 66.8 us -> 1.42 us
  other arithmetic: 40.7 us -> 0 us
  blocking collectives: 26.9 us -> 0 us
  starting transfers between devices: 17.9 us -> 0 us
    ppermute x14 -> x0, waiting for transfers between devices: 389 us -> none  [visit_block(): held_kv = lax.ppermute(held_kv, 'cp', send_pairs)]
    dot_general x27 -> x0, matrix products: 176 us -> none  [the longest x8 72.9 us: block_stats(): jnp.einsum('bhqk,bkhe->bhqe', weights.astype(jnp.bfloat16), value_rows, p...]
    pallas_call x0 -> x1, Pallas kernels: none -> 108 us  [device_step(): pl.pallas_call(functools.partial(kernel, (n, per, heads, head_dim, width,...]
    while x28 -> x0, local copies, waits for them, and re-layouts: 63 us -> none
    reduce_sum x16 -> x0, other arithmetic: 38.6 us -> none  [the longest x8 28.2 us: block_stats(): return (row_max, jnp.sum(weights, axis=-1), value_sum)]
    all_gather x1 -> x0, blocking collectives: 26.9 us -> none  [device_step(): gathered = lax.all_gather(local_stats, 'cp')]
    ppermute x14 -> x0, starting transfers between devices: 17.9 us -> none  [visit_block(): held_kv = lax.ppermute(held_kv, 'cp', send_pairs)]
  transfers between devices with their start and end apart: 14 -> 0, of which waited for: 14 -> 0; matrix products, arithmetic and copies ran while one was open for 12% -> 0% of each run, Pallas kernels for 0% -> 0%
where the time goes in v1:
time: 109 us
  Pallas kernels  108 us (99%)
  local copies, waits for them, and re-layouts  1.42 us (1%)
    pallas_call x1, Pallas kernels, device_step(): pl.pallas_call(functools.partial(kernel, (n, per, heads, head_dim, width,...  108 us

profile of v1, /device:TPU:113, one launch (start us, length us, event | category | flops | bytes accessed | tf_op | source)
XLA Modules:
  0.0 109.3 jit_solution(10096697296677326837)
XLA Ops:
  0.0 107.9 %encoder_pool.1 = f32[16,768]{1,0:T(8,128)} custom-call(bf16[16,128,768]{2,1,0:T(8,128)(2,1)} %images.1, bf16[2304,768]{1,0:T(8,128)(2,1)} %bitcast.12, bf16[768,768]{1,0:T(8,128)(2,1)} %bitcast.14, bf16[768,3072]{1,0:T(8,128)(2,1)} %wup_h.1, bf16[3072,768]{1,0:T(8,128)(2,1)} %wdown_h.1, bf16[1536,768]{1,0:T(8,128)(2,1)} %bitcast.13, ...), custom_call_target="tpu_custom_call" | custom-call | tf_op jit(solution)/shard_map/encoder_pool/pallas_call | solution.py:355
  107.9 1.4 %copy.30 = f32[16,768]{1,0:T(8,128)} copy(f32[16,768]{1,0:T(8,128)} %encoder_pool.1) | data formatting | bytes 98304

commit v2 on v1

--- a/solution.py
+++ b/solution.py
@@ -44,9 +44,9 @@
     (probe_h, out_ref,
            wqkv, wout, wup, wdown, wpkv, wpq, pwout, pwup, pwdown,
            xbuf, qz, kbuf, vt, s00, s01, s10, s11, p00, p01, p10, p11, mbuf, ctx, hbuf, rbuf, nbuf, hid, zbuf,
-           score, pvbuf, ubuf, cols, abuf, gath, vecs, probe, *tail_refs) = rest[N_SMALL:]
+           score, pvbuf, ubuf, cols, abuf, gath, rel, vecs, probe, *tail_refs) = rest[N_SMALL:]
     small_bufs = tail_refs[:N_SMALL]
-    send_sem, recv_sem, w_sem, gsend_sem, grecv_sem, v_sem = tail_refs[N_SMALL:]
+    send_sem, recv_sem, rel_sem, fwd_sem, w_sem, gsend_sem, grecv_sem, v_sem = tail_refs[N_SMALL:]
     run = images.shape[1]
     tokens = n * run
     nch = n // 2
@@ -82,22 +82,42 @@
         if nch - d != d:
             deltas.append(nch - d)
 
+    def remote(src, dst, send, recv, device):
+        return pltpu.make_async_remote_copy(
+            src_ref=src, dst_ref=dst, send_sem=send, recv_sem=recv, device_id={"cp": device}, device_id_type=pl.DeviceIdType.MESH)
+
+    relayed = nch == 4
+
+    def chip_core(delta, c):
+        return ((own + delta + nch) % nch) * 2 + c
+
     def sends(j):
         copies = []
+
+        def add(block, dst, recv, device):
+            copies.append(remote(images.at[block * per + j], dst, send_sem.at[j, len(copies)], recv, device))
+
+        for up in (0, 1) if relayed else ():
+            add(chip_core(2, up), rel.at[j, up], rel_sem.at[j, up], chip_core(1 - 2 * up, core))
         for delta in deltas:
             for cc in (0, 1):
-                if delta == 0 and cc == 0:
+                if (delta == 0 and cc == 0) or (relayed and delta == 2):
                     continue
-                dst = ((own + delta) % nch) * 2 + (core + cc) % 2
-                copies.append(pltpu.make_async_remote_copy(
-                    src_ref=images.at[dst * per + j],
-                    dst_ref=xbuf.at[j, me],
-                    send_sem=send_sem.at[j, len(copies)],
-                    recv_sem=recv_sem.at[j, me],
-                    device_id={"cp": dst},
-                    device_id_type=pl.DeviceIdType.MESH,
-                ))
+                dst = chip_core(delta, (core + cc) % 2)
+                add(dst, xbuf.at[j, me], recv_sem.at[j, me], dst)
         return copies
+
+    def forwards(j):
+        copies = []
+        for up in (0, 1) if relayed else ():
+            source = chip_core(2 * up - 1, core)
+            copies.append(remote(rel.at[j, up], xbuf.at[j, source], fwd_sem.at[j, up], recv_sem.at[j, source], chip_core(1 - 2 * up, up)))
+        return copies
+
+    def start_forwards(j):
+        for up, copy in enumerate(forwards(j)):
+            pltpu.make_async_copy(images.at[0], rel.at[j, up], rel_sem.at[j, up]).wait()
+            copy.start()
 
     small_copies = [pltpu.make_async_copy(src, dst, v_sem.at[i]) for i, (src, dst) in enumerate(zip((*smalls, probe_h), (*small_bufs, probe)))]
     start_weight(0)
@@ -111,9 +131,8 @@
         pl.semaphore_signal(barrier, inc=1, device_id={"cp": (me + s) % n}, device_id_type=pl.DeviceIdType.MESH)
     pl.semaphore_wait(barrier, n - 1)
 
-    for j in range(per):
-        for copy in sends(j):
-            copy.start()
+    for copy in sends(0):
+        copy.start()
     for i in range(1, len(weights)):
         start_weight(i)
 
@@ -151,6 +170,14 @@
 
     def one_image(j, carry):
         for delta in deltas:
+            if delta == 1:
+                @pl.when(j == 0)
+                def _():
+                    start_forwards(0)
+                    for later in range(1, per):
+                        for copy in sends(later):
+                            copy.start()
+
             chip = (own + delta) % nch
             wait_source(j, chip * 2)
             wait_source(j, chip * 2 + 1)
@@ -205,6 +232,8 @@
 
         @pl.when(j == 0)
         def _():
+            for later in range(1, per):
+                start_forwards(later)
             for i in range(1, 6):
                 wait_weight(i)
             q16 = jnp.broadcast_to(probe[...], (16, width))
@@ -290,7 +319,7 @@
     for copy in copies:
         copy.start()
     for j in range(per):
-        for copy in sends(j):
+        for copy in sends(j) + forwards(j):
             copy.wait_send()
     for s in range(1, n):
         src = (me + s) % n
@@ -342,11 +371,14 @@
             pltpu.VMEM((3, width, LANES), F32),
             pltpu.VMEM((16, width), F32),
             pltpu.VMEM((n, 8, width), F32),
+            pltpu.VMEM((per, 2, run, width), BF16),
             pltpu.VMEM((N_FIXED + 2 * mlp // width, width), F32),
             pltpu.VMEM(pool_probe.shape, BF16),
             *[pltpu.VMEM(v.shape, F32) for v in smalls],
             pltpu.SemaphoreType.DMA((per, n)),
             pltpu.SemaphoreType.DMA((per, n)),
+            pltpu.SemaphoreType.DMA((per, 2)),
+            pltpu.SemaphoreType.DMA((per, 2)),
             pltpu.SemaphoreType.DMA((len(big) - 1,)),
             pltpu.SemaphoreType.DMA((n,)),
             pltpu.SemaphoreType.DMA((n,)),

time: 109 us -> 108 us (level)
  Pallas kernels: 108 us -> 106 us
    pallas_call x1, Pallas kernels: 108 us -> 106 us  [device_step(): pl.pallas_call(functools.partial(kernel, (n, per, heads, head_dim, width,...]
where the time goes in v2:
time: 108 us
  Pallas kernels  106 us (98%)
  local copies, waits for them, and re-layouts  1.42 us (1%)
    pallas_call x1, Pallas kernels, device_step(): pl.pallas_call(functools.partial(kernel, (n, per, heads, head_dim, width,...  106 us

profile of v2, /device:TPU:113, one launch (start us, length us, event | category | flops | bytes accessed | tf_op | source)
XLA Modules:
  0.0 107.8 jit_solution(3746789962999261797)
XLA Ops:
  0.0 106.3 %encoder_pool.1 = f32[16,768]{1,0:T(8,128)} custom-call(bf16[16,128,768]{2,1,0:T(8,128)(2,1)} %images.1, bf16[2304,768]{1,0:T(8,128)(2,1)} %bitcast.12, bf16[768,768]{1,0:T(8,128)(2,1)} %bitcast.14, bf16[768,3072]{1,0:T(8,128)(2,1)} %wup_h.1, bf16[3072,768]{1,0:T(8,128)(2,1)} %wdown_h.1, bf16[1536,768]{1,0:T(8,128)(2,1)} %bitcast.13, ...), custom_call_target="tpu_custom_call" | custom-call | tf_op jit(solution)/shard_map/encoder_pool/pallas_call | solution.py:387
  106.3 1.4 %copy.30 = f32[16,768]{1,0:T(8,128)} copy(f32[16,768]{1,0:T(8,128)} %encoder_pool.1) | data formatting | bytes 98304

commit v3 on v2

--- a/solution.py
+++ b/solution.py
@@ -11,6 +11,7 @@
 EPSILON = 1e-6
 LANES = 128
 BLOCK = 256
+UNROLL = 4
 F32 = jnp.float32
 BF16 = jnp.bfloat16
 
@@ -36,6 +37,11 @@
 
 def dot_t(a, b):
     return lax.dot_general(a, b, (((1,), (1,)), ((), ())), preferred_element_type=F32)
+
+
+def halves_t(a_ref, lo, size, b):
+    half = size // 2
+    return [(r, half, dot_t(a_ref[lo + r:lo + r + half, :], b)) for r in (0, half)]
 
 
 def kernel(cfg, images, wqkv_h, wout_h, wup_h, wdown_h, wpkv_h, wpq_h, pwout_h, pwup_h, pwdown_h, *rest):
@@ -169,29 +175,52 @@
     p_refs = ((p00, p01), (p10, p11))
 
     def one_image(j, carry):
-        for delta in deltas:
-            if delta == 1:
-                @pl.when(j == 0)
-                def _():
+        def chip_of(k):
+            return (own + deltas[k]) % nch
+
+        def enter(k):
+            x = xbuf[j, pl.ds(chip_of(k) * 2, 2)].reshape(BLOCK, width)
+            for r0 in range(0, BLOCK, 64):
+                hbuf[k % 2, r0:r0 + 64, :] = layer_norm(x[r0:r0 + 64].astype(F32), vec(LN1_G), vec(LN1_B)).astype(BF16)
+
+        def project(k):
+            tok = pl.multiple_of(chip_of(k) * BLOCK, BLOCK)
+            h = hbuf[k % 2]
+            for r, size, qt in halves_t(wqkv, 0, width, h):
+                qt = (qt + col_bias(0, r, size)).astype(BF16)
+                for h0 in range(0, size, head_dim):
+                    hd = (r + h0) // head_dim
+                    off = (hd % 2) * head_dim
+                    qz[hd, off:off + head_dim, pl.ds(tok, BLOCK)] = qt[h0:h0 + head_dim]
+            for r, size, v in halves_t(wqkv, 2 * width, width, h):
+                vt[r:r + size, pl.ds(tok, BLOCK)] = (v + col_bias(1, r, size)).astype(BF16)
+            kbuf[pl.ds(tok, BLOCK), :] = (dot_t(h, wqkv[width:2 * width, :]) + vec(B_K)).astype(BF16)
+
+        def wait_chip(k):
+            wait_source(j, chip_of(k) * 2)
+            wait_source(j, chip_of(k) * 2 + 1)
+
+        @pl.when(j == 0)
+        def _():
+            for k in range(nch):
+                if k == 1:
                     start_forwards(0)
                     for later in range(1, per):
                         for copy in sends(later):
                             copy.start()
-
-            chip = (own + delta) % nch
-            wait_source(j, chip * 2)
-            wait_source(j, chip * 2 + 1)
-            tok = pl.multiple_of(chip * BLOCK, BLOCK)
-            x = xbuf[j, pl.ds(chip * 2, 2)].reshape(BLOCK, width)
-            for r0 in range(0, BLOCK, 64):
-                hbuf[r0:r0 + 64, :] = layer_norm(x[r0:r0 + 64].astype(F32), vec(LN1_G), vec(LN1_B)).astype(BF16)
-            h = hbuf[...]
-            kbuf[pl.ds(tok, BLOCK), :] = (dot_t(h, wqkv[width:2 * width, :]) + vec(B_K)).astype(BF16)
-            qt = (dot_t(wqkv[0:width, :], h) + col_bias(0, 0, width)).astype(BF16)
-            for hd in range(heads):
-                off = (hd % 2) * head_dim
-                qz[hd, off:off + head_dim, pl.ds(tok, BLOCK)] = qt[hd * head_dim:(hd + 1) * head_dim]
-            vt[:, pl.ds(tok, BLOCK)] = (dot_t(wqkv[2 * width:3 * width, :], h) + col_bias(1, 0, width)).astype(BF16)
+                wait_chip(k)
+                enter(k)
+                project(k)
+
+        @pl.when(j > 0)
+        def _():
+            for k in range(nch):
+                wait_chip(k)
+            enter(0)
+            for k in range(nch):
+                if k + 1 < nch:
+                    enter(k + 1)
+                project(k)
 
         def qk(step, slot):
             hp, qb = step // nq, step % nq
@@ -222,13 +251,12 @@
         qk(0, 0)
 
         def attend(i, c):
-            qk(2 * i + 1, 1)
-            softmax_pv(2 * i, 0)
-            qk((2 * i + 2) % nsteps, 0)
-            softmax_pv(2 * i + 1, 1)
+            for k in range(UNROLL):
+                qk((UNROLL * i + k + 1) % nsteps, (k + 1) % 2)
+                softmax_pv(UNROLL * i + k, k % 2)
             return c
 
-        lax.fori_loop(0, nsteps // 2, attend, 0)
+        lax.fori_loop(0, nsteps // UNROLL, attend, 0)
 
         @pl.when(j == 0)
         def _():
@@ -242,6 +270,13 @@
             col = lax.broadcasted_iota(jnp.int32, (16, width), 1)
             ubuf[...] = jnp.where(col // head_dim == row, u, 0.0).astype(BF16)
 
+        def pool(t, block):
+            z = zbuf[t]
+            start = pl.multiple_of((block % nq) * BLOCK, BLOCK)
+            parts = [(pk + col_bias(2, r, size)).astype(BF16) for r, size, pk in halves_t(wpkv, 0, width, z)]
+            score[:, pl.ds(start, BLOCK)] = dot(ubuf[...], jnp.concatenate(parts, axis=0))
+            pvbuf[pl.ds(start, BLOCK), :] = (dot_t(z, wpkv[width:2 * width, :]) + vec(P_BV)).astype(BF16)
+
         def tail(i, c):
             starts = [pl.multiple_of((2 * i + t) * BLOCK, BLOCK) for t in (0, 1)]
 
@@ -265,25 +300,21 @@
                 for r0 in range(0, BLOCK, 64):
                     zbuf[t, r0:r0 + 64, :] = layer_norm(y[r0:r0 + 64].astype(F32), vec(LNF_G), vec(LNF_B)).astype(BF16)
 
-            def pool(t):
-                z = zbuf[t]
-                pk = (dot_t(wpkv[0:width, :], z) + col_bias(2, 0, width)).astype(BF16)
-                score[:, pl.ds(starts[t], BLOCK)] = dot(ubuf[...], pk)
-                pvbuf[pl.ds(starts[t], BLOCK), :] = (dot_t(z, wpkv[width:2 * width, :]) + vec(P_BV)).astype(BF16)
-
             resid(0)
             resid(1)
+            pool(1, 2 * i + nq - 1)
             norm(0)
             up(0)
             norm(1)
             down(0)
             up(1)
-            pool(0)
+            pool(0, 2 * i)
             down(1)
-            pool(1)
             return c
 
+        zbuf[1] = jnp.zeros((BLOCK, width), BF16)
         lax.fori_loop(0, nq // 2, tail, 0)
+        pool(1, nq - 1)
 
         s = score[...]
         w = jnp.exp2((s - jnp.max(s, axis=-1, keepdims=True)) * exp_scale)
@@ -360,7 +391,7 @@
             *[pltpu.VMEM((tokens, BLOCK), BF16) for _ in range(4)],
             pltpu.VMEM((2, 2, 8, BLOCK), F32),
             pltpu.VMEM((tokens, width), BF16),
-            pltpu.VMEM((BLOCK, width), BF16),
+            pltpu.VMEM((2, BLOCK, width), BF16),
             pltpu.VMEM((2, BLOCK, width), BF16),
             pltpu.VMEM((2, BLOCK, width), BF16),
             pltpu.VMEM((2, BLOCK, mlp), BF16),

time: 108 us -> 105 us (0.972)
  Pallas kernels: 106 us -> 104 us
    pallas_call x1, Pallas kernels: 106 us -> 104 us  [device_step(): pl.pallas_call(functools.partial(kernel, (n, per, heads, head_dim, width,...]
where the time goes in v3:
time: 105 us
  Pallas kernels  104 us (99%)
  local copies, waits for them, and re-layouts  1.42 us (1%)
    pallas_call x1, Pallas kernels, device_step(): pl.pallas_call(functools.partial(kernel, (n, per, heads, head_dim, width,...  104 us

profile of v3, /device:TPU:113, one launch (start us, length us, event | category | flops | bytes accessed | tf_op | source)
XLA Modules:
  0.0 105.1 jit_solution(11403962866376022770)
XLA Ops:
  0.0 103.6 %encoder_pool.1 = f32[16,768]{1,0:T(8,128)} custom-call(bf16[16,128,768]{2,1,0:T(8,128)(2,1)} %images.1, bf16[2304,768]{1,0:T(8,128)(2,1)} %bitcast.12, bf16[768,768]{1,0:T(8,128)(2,1)} %bitcast.14, bf16[768,3072]{1,0:T(8,128)(2,1)} %wup_h.1, bf16[3072,768]{1,0:T(8,128)(2,1)} %wdown_h.1, bf16[1536,768]{1,0:T(8,128)(2,1)} %bitcast.13, ...), custom_call_target="tpu_custom_call" | custom-call | tf_op jit(solution)/shard_map/encoder_pool/pallas_call | solution.py:418
  103.6 1.4 %copy.30 = f32[16,768]{1,0:T(8,128)} copy(f32[16,768]{1,0:T(8,128)} %encoder_pool.1) | data formatting | bytes 98304

commit v4 on v3

--- a/solution.py
+++ b/solution.py
@@ -158,7 +158,7 @@
         span = slice(hc * width, (hc + 1) * width)
         vecs[N_FIXED + hc:N_FIXED + hc + 1, :] = bup_b[span].reshape(1, width)
         vecs[N_FIXED + hid_chunks + hc:N_FIXED + hid_chunks + hc + 1, :] = pbup_b[span].reshape(1, width)
-    for slot, row in enumerate((B_Q, B_V, P_BK)):
+    for slot, row in enumerate((B_Q, B_V)):
         cols[slot] = jnp.transpose(jnp.broadcast_to(vec(row), (LANES, width)))
     qz[...] = jnp.zeros_like(qz)
     abuf[...] = jnp.zeros_like(abuf)
@@ -271,11 +271,10 @@
             ubuf[...] = jnp.where(col // head_dim == row, u, 0.0).astype(BF16)
 
         def pool(t, block):
-            z = zbuf[t]
             start = pl.multiple_of((block % nq) * BLOCK, BLOCK)
-            parts = [(pk + col_bias(2, r, size)).astype(BF16) for r, size, pk in halves_t(wpkv, 0, width, z)]
-            score[:, pl.ds(start, BLOCK)] = dot(ubuf[...], jnp.concatenate(parts, axis=0))
-            pvbuf[pl.ds(start, BLOCK), :] = (dot_t(z, wpkv[width:2 * width, :]) + vec(P_BV)).astype(BF16)
+            kv = dot_t(zbuf[t], wpkv[...])
+            score[:, pl.ds(start, BLOCK)] = dot_t(ubuf[...], (kv[:, 0:width] + vec(P_BK)).astype(BF16))
+            pvbuf[pl.ds(start, BLOCK), :] = (kv[:, width:2 * width] + vec(P_BV)).astype(BF16)
 
         def tail(i, c):
             starts = [pl.multiple_of((2 * i + t) * BLOCK, BLOCK) for t in (0, 1)]
@@ -295,10 +294,16 @@
                     cols_ = slice(hc * width, (hc + 1) * width)
                     hid[t, :, cols_] = gelu(dot(nbuf[t], wup[:, cols_]) + vec(N_FIXED + hc)).astype(BF16)
 
-            def down(t):
-                y = (rbuf[t].astype(F32) + dot(hid[t], wdown[...]) + vec(B_DOWN)).astype(BF16)
-                for r0 in range(0, BLOCK, 64):
-                    zbuf[t, r0:r0 + 64, :] = layer_norm(y[r0:r0 + 64].astype(F32), vec(LNF_G), vec(LNF_B)).astype(BF16)
+            def down(t, row_parts):
+                for lo, size, parts in row_parts:
+                    rows = slice(lo, lo + size)
+                    y = jnp.concatenate([dot(hid[t, rows, :], wdown[:, c0:c1]) for c0, c1 in parts], axis=1)
+                    y = (rbuf[t, rows, :].astype(F32) + y + vec(B_DOWN)).astype(BF16)
+                    for r0 in range(0, size, 64):
+                        zbuf[t, lo + r0:lo + r0 + 64, :] = layer_norm(y[r0:r0 + 64].astype(F32), vec(LNF_G), vec(LNF_B)).astype(BF16)
+
+            whole = [(0, width)]
+            row_halves = [(0, BLOCK // 2, whole), (BLOCK // 2, BLOCK // 2, whole)]
 
             resid(0)
             resid(1)
@@ -306,10 +311,10 @@
             norm(0)
             up(0)
             norm(1)
-            down(0)
             up(1)
+            down(0, [(0, BLOCK, whole)])
+            down(1, row_halves)
             pool(0, 2 * i)
-            down(1)
             return c
 
         zbuf[1] = jnp.zeros((BLOCK, width), BF16)
@@ -399,7 +404,7 @@
             pltpu.VMEM((16, tokens), F32),
             pltpu.VMEM((tokens, width), BF16),
             pltpu.VMEM((16, width), BF16),
-            pltpu.VMEM((3, width, LANES), F32),
+            pltpu.VMEM((2, width, LANES), F32),
             pltpu.VMEM((16, width), F32),
             pltpu.VMEM((n, 8, width), F32),
             pltpu.VMEM((per, 2, run, width), BF16),

time: 105 us -> 102 us (0.971)
  Pallas kernels: 104 us -> 101 us
    pallas_call x1, Pallas kernels: 104 us -> 101 us  [device_step(): pl.pallas_call(functools.partial(kernel, (n, per, heads, head_dim, width,...]
where the time goes in v4:
time: 102 us
  Pallas kernels  101 us (99%)
  local copies, waits for them, and re-layouts  1.42 us (1%)
    pallas_call x1, Pallas kernels, device_step(): pl.pallas_call(functools.partial(kernel, (n, per, heads, head_dim, width,...  101 us

profile of v4, /device:TPU:113, one launch (start us, length us, event | category | flops | bytes accessed | tf_op | source)
XLA Modules:
  0.0 101.9 jit_solution(12848746692703218825)
XLA Ops:
  0.0 100.5 %encoder_pool.1 = f32[16,768]{1,0:T(8,128)} custom-call(bf16[16,128,768]{2,1,0:T(8,128)(2,1)} %images.1, bf16[2304,768]{1,0:T(8,128)(2,1)} %bitcast.12, bf16[768,768]{1,0:T(8,128)(2,1)} %bitcast.14, bf16[768,3072]{1,0:T(8,128)(2,1)} %wup_h.1, bf16[3072,768]{1,0:T(8,128)(2,1)} %wdown_h.1, bf16[1536,768]{1,0:T(8,128)(2,1)} %bitcast.13, ...), custom_call_target="tpu_custom_call" | custom-call | tf_op jit(solution)/shard_map/encoder_pool/pallas_call | solution.py:423
  100.5 1.4 %copy.30 = f32[16,768]{1,0:T(8,128)} copy(f32[16,768]{1,0:T(8,128)} %encoder_pool.1) | data formatting | bytes 98304

commit v5 on v4

--- a/solution.py
+++ b/solution.py
@@ -11,7 +11,7 @@
 EPSILON = 1e-6
 LANES = 128
 BLOCK = 256
-UNROLL = 4
+UNROLL = 8
 F32 = jnp.float32
 BF16 = jnp.bfloat16
 
@@ -139,7 +139,7 @@
 
     for copy in sends(0):
         copy.start()
-    for i in range(1, len(weights)):
+    for i in (2, 1, *range(3, len(weights))):
         start_weight(i)
 
     for copy in small_copies:
@@ -162,6 +162,7 @@
         cols[slot] = jnp.transpose(jnp.broadcast_to(vec(row), (LANES, width)))
     qz[...] = jnp.zeros_like(qz)
     abuf[...] = jnp.zeros_like(abuf)
+    zbuf[1] = jnp.zeros((BLOCK, width), BF16)
     wait_weight(0)
 
     def col_bias(slot, lo, size):
@@ -173,6 +174,28 @@
 
     s_refs = ((s00, s01), (s10, s11))
     p_refs = ((p00, p01), (p10, p11))
+
+    def pool(t, block):
+        start = pl.multiple_of((block % nq) * BLOCK, BLOCK)
+        kv = dot_t(zbuf[t], wpkv[...])
+        score[:, pl.ds(start, BLOCK)] = dot_t(ubuf[...], (kv[:, 0:width] + vec(P_BK)).astype(BF16))
+        pvbuf[pl.ds(start, BLOCK), :] = (kv[:, width:2 * width] + vec(P_BV)).astype(BF16)
+
+    def pool_query():
+        q16 = jnp.broadcast_to(probe[...], (16, width))
+        u = dot_t(q16, wpq[...]) + vec(P_BQ)
+        row = lax.broadcasted_iota(jnp.int32, (16, width), 0)
+        col = lax.broadcasted_iota(jnp.int32, (16, width), 1)
+        ubuf[...] = jnp.where(col // head_dim == row, u, 0.0).astype(BF16)
+
+    def finish_pool(image):
+        pool(1, nq - 1)
+        s = score[...]
+        w = jnp.exp2((s - jnp.max(s, axis=-1, keepdims=True)) * exp_scale)
+        a = dot(w.astype(BF16), pvbuf[...]) / jnp.sum(w, axis=-1, keepdims=True)
+        row = lax.broadcasted_iota(jnp.int32, (16, width), 0)
+        col = lax.broadcasted_iota(jnp.int32, (16, width), 1)
+        abuf[pl.ds(image, 1), :] = jnp.sum(jnp.where(col // head_dim == row, a, 0.0), axis=0, keepdims=True)
 
     def one_image(j, carry):
         def chip_of(k):
@@ -208,6 +231,8 @@
                     for later in range(1, per):
                         for copy in sends(later):
                             copy.start()
+                    wait_weight(2)
+                    pool_query()
                 wait_chip(k)
                 enter(k)
                 project(k)
@@ -216,6 +241,7 @@
         def _():
             for k in range(nch):
                 wait_chip(k)
+            finish_pool(j - 1)
             enter(0)
             for k in range(nch):
                 if k + 1 < nch:
@@ -262,19 +288,8 @@
         def _():
             for later in range(1, per):
                 start_forwards(later)
-            for i in range(1, 6):
+            for i in (1, 3, 4, 5):
                 wait_weight(i)
-            q16 = jnp.broadcast_to(probe[...], (16, width))
-            u = dot_t(q16, wpq[...]) + vec(P_BQ)
-            row = lax.broadcasted_iota(jnp.int32, (16, width), 0)
-            col = lax.broadcasted_iota(jnp.int32, (16, width), 1)
-            ubuf[...] = jnp.where(col // head_dim == row, u, 0.0).astype(BF16)
-
-        def pool(t, block):
-            start = pl.multiple_of((block % nq) * BLOCK, BLOCK)
-            kv = dot_t(zbuf[t], wpkv[...])
-            score[:, pl.ds(start, BLOCK)] = dot_t(ubuf[...], (kv[:, 0:width] + vec(P_BK)).astype(BF16))
-            pvbuf[pl.ds(start, BLOCK), :] = (kv[:, width:2 * width] + vec(P_BV)).astype(BF16)
 
         def tail(i, c):
             starts = [pl.multiple_of((2 * i + t) * BLOCK, BLOCK) for t in (0, 1)]
@@ -317,19 +332,11 @@
             pool(0, 2 * i)
             return c
 
-        zbuf[1] = jnp.zeros((BLOCK, width), BF16)
         lax.fori_loop(0, nq // 2, tail, 0)
-        pool(1, nq - 1)
-
-        s = score[...]
-        w = jnp.exp2((s - jnp.max(s, axis=-1, keepdims=True)) * exp_scale)
-        a = dot(w.astype(BF16), pvbuf[...]) / jnp.sum(w, axis=-1, keepdims=True)
-        row = lax.broadcasted_iota(jnp.int32, (16, width), 0)
-        col = lax.broadcasted_iota(jnp.int32, (16, width), 1)
-        abuf[pl.ds(j, 1), :] = jnp.sum(jnp.where(col // head_dim == row, a, 0.0), axis=0, keepdims=True)
         return carry
 
     lax.fori_loop(0, per, one_image, 0)
+    finish_pool(per - 1)
 
     for i in range(6, len(weights)):
         wait_weight(i)

time: 102 us -> 99.5 us (0.975)
  Pallas kernels: 101 us -> 97.9 us
    pallas_call x1, Pallas kernels: 101 us -> 97.9 us  [device_step(): pl.pallas_call(functools.partial(kernel, (n, per, heads, head_dim, width,...]
where the time goes in v5:
time: 99.5 us; the launch traced here: 99.4 us
  Pallas kernels  97.9 us (98%)
  local copies, waits for them, and re-layouts  1.42 us (1%)
    pallas_call x1, Pallas kernels, device_step(): pl.pallas_call(functools.partial(kernel, (n, per, heads, head_dim, width,...  97.9 us

profile of v5, /device:TPU:113, one launch (start us, length us, event | category | flops | bytes accessed | tf_op | source)
XLA Modules:
  0.0 99.4 jit_solution(10677517185621205079)
XLA Ops:
  0.0 97.9 %encoder_pool.1 = f32[16,768]{1,0:T(8,128)} custom-call(bf16[16,128,768]{2,1,0:T(8,128)(2,1)} %images.1, bf16[2304,768]{1,0:T(8,128)(2,1)} %bitcast.12, bf16[768,768]{1,0:T(8,128)(2,1)} %bitcast.14, bf16[768,3072]{1,0:T(8,128)(2,1)} %wup_h.1, bf16[3072,768]{1,0:T(8,128)(2,1)} %wdown_h.1, bf16[1536,768]{1,0:T(8,128)(2,1)} %bitcast.13, ...), custom_call_target="tpu_custom_call" | custom-call | tf_op jit(solution)/shard_map/encoder_pool/pallas_call | solution.py:430
  97.9 1.4 %copy.30 = f32[16,768]{1,0:T(8,128)} copy(f32[16,768]{1,0:T(8,128)} %encoder_pool.1) | data formatting | bytes 98304
